TPU v7x, 32 devices: a whole 2x2x4 slice. The times are simulated.
32 devices in a mesh: role: 2 (over core), rep: 4 (over z), tp: 4 (over y, x).
Axes of the slice: x: 2, y: 2, z: 4, core: 2. Of those that a mesh axis runs over, the one named last changes fastest.
Arguments:
- pre_act: bfloat16 [2, 2, 64, 14784], P('role', None, 'rep', 'tp'), may hold values from -6 to 6
- next_pre: bfloat16 [2, 2, 64, 14784], P('role', None, 'rep', 'tp'), may hold values from -6 to 6
- stream: bfloat16 [2, 2, 64, 8192], P('role', None, 'tp', 'rep'), may hold values from -6 to 6
- cotangent: bfloat16 [64, 8192], P('tp', 'rep'), may hold values from -6 to 6
- weights: float32 [2, 14784, 8192], P('role', 'tp', 'rep'), may hold values from -6 to 6
- first_moment: float32 [14784, 8192], P('tp', 'rep'), may hold values from -0.18 to 0.18
- second_moment: float32 [14784, 8192], P('tp', 'rep'), may hold values from 0.0001 to 0.001
- tree_parent: int32 [2, 64], P('role', 'tp'), may hold values from 0 to 63, as said below
- tree_depth: int32 [2, 64], P('role', 'tp'), may hold values from 1 to 16, as said below
Outputs:
- first_out: bfloat16 [2, 64, 8192], P('role', 'tp', 'rep')
- next_out: bfloat16 [2, 64, 8192], P('role', 'tp', 'rep')
- new_weights: float32 [2, 14784, 8192], P('role', 'tp', 'rep')
Inputs may be any that keep to these rules, and one draw needn't show every extreme that they name: `tree_parent`: each entry names a first-pass row of the same group that lies in the same aligned block of 16 rows as the entry's own row. `tree_depth`: one more than the depth of the named parent in its block's first-pass tree; in that tree every row but the block's first names an earlier row of the block as parent, and the first row has depth 0.
All inputs are finite; a program needn't handle non-finite values.
Results may differ from a plain program's by a relative error of at most 0.0041.
Values may be sent and summed in bfloat16 or wider, within the bound.
No kernel may reach another device: no remote copies, remote signals or barrier semaphores. Data moves between devices by JAX's collectives and lax.ppermute only.
A program may use at most 256 MiB of HBM per device.

v0:
```python
import jax
import jax.numpy as jnp
from jax import lax
from jax.sharding import PartitionSpec as P

FF = 14784
beta_one = 0.9
beta_two = 0.95
epsilon = 1e-08
learn_rate = 0.08
decay_rate = 0.1
correct_one = 1.0 - 0.9**60
correct_two = 1.0 - 0.95**60


def shifted(value, axis, by):
    size = lax.axis_size(axis)
    pairs = [(i, i + by) for i in range(size) if 0 <= i + by < size]
    return lax.ppermute(value, axis, pairs)


def activate(both_halves):
    return (
        jax.nn.silu(both_halves[0].astype(jnp.float32)) * both_halves[1].astype(jnp.float32)
    ).astype(jnp.bfloat16)


def adam_step(master, moment_one, moment_two, gradient):
    moment_one = beta_one * moment_one + (1.0 - beta_one) * gradient
    moment_two = beta_two * moment_two + (1.0 - beta_two) * gradient * gradient
    direction = moment_one / correct_one / (jnp.sqrt(moment_two / correct_two) + epsilon)
    return master - learn_rate * (direction + decay_rate * master)


def local(
    pre_act,
    next_pre,
    stream,
    cotangent,
    weights,
    first_moment,
    second_moment,
    tree_parent,
    tree_depth,
):
    learner = lax.axis_index("role") == 0
    factor = FF ** (-0.5)
    hidden = activate(pre_act[0])
    upcoming = activate(next_pre[0])
    older = weights[0].astype(jnp.bfloat16)
    cot_rows = lax.all_gather(cotangent, "tp", axis=0, tiled=True)
    width_ff, width_d = older.shape
    empty_grad = jnp.zeros((width_ff, width_d), jnp.float32)
    gradient = empty_grad
    segment = lax.all_gather(hidden, "rep", axis=0, tiled=True)
    piece = segment
    contribute_partial_value = piece

    def accumulate(held_sum):
        return lax.dot_general(
            segment, cot_rows, (((0,), (0,)), ((), ())), preferred_element_type=jnp.float32
        )

    gradient = lax.cond(learner, accumulate, lambda held_sum: held_sum, gradient)
    partial_value, gradient = (contribute_partial_value, gradient)
    summed = lax.psum_scatter(
        jnp.dot(partial_value, older, preferred_element_type=jnp.float32),
        "tp",
        scatter_dimension=0,
        tiled=True,
    )
    first_out = (stream[0, 0].astype(jnp.float32) + factor * summed).astype(jnp.bfloat16)
    updated = adam_step(weights[0], first_moment, second_moment, factor * gradient)
    fresh = updated.astype(jnp.bfloat16)
    pushed = shifted(fresh, "role", 1)
    current = jnp.where(learner, fresh, pushed)
    new_weights = jnp.where(learner, updated, pushed.astype(jnp.float32))
    piece = lax.all_gather(upcoming, "rep", axis=0, tiled=True)
    next_summed = lax.psum_scatter(
        jnp.dot(piece, current, preferred_element_type=jnp.float32),
        "tp",
        scatter_dimension=0,
        tiled=True,
    )
    block_rows = first_out.shape[0]
    local_parent = tree_parent[0] - lax.axis_index("tp") * block_rows
    onehot = (local_parent[:, None] == jnp.arange(block_rows, dtype=jnp.int32)[None, :]).astype(
        jnp.bfloat16
    )
    picked = jnp.dot(onehot, first_out, preferred_element_type=jnp.float32)
    portion = 1.0 / (1.0 + tree_depth[0].astype(jnp.float32))
    total = stream[0, 1].astype(jnp.float32) + factor * next_summed + picked * portion[:, None]
    next_out = total.astype(jnp.bfloat16)
    return (first_out[None], next_out[None], new_weights[None])


def solution(mesh):
    placed = (
        P("role", None, "rep", "tp"),
        P("role", None, "rep", "tp"),
        P("role", None, "tp", "rep"),
        P("tp", "rep"),
        P("role", "tp", "rep"),
        P("tp", "rep"),
        P("tp", "rep"),
        P("role", "tp"),
        P("role", "tp"),
    )
    return jax.shard_map(
        local,
        mesh=mesh,
        in_specs=placed,
        out_specs=(P("role", "tp", "rep"), P("role", "tp", "rep"), P("role", "tp", "rep")),
        check_vma=False,
    )
```

profile of v0, /device:TPU:0, one launch (start us, length us, event | category | flops | bytes accessed | tf_op | source)
XLA Modules:
  0.0 193.4 jit_solution(9640457482474888950)
XLA Ops:
  7.2 0.0 reduce-scatter.3.cloned.1.call-start
  7.2 1.0 fusion.15
  8.3 16.9 %all_gather.9 = bf16[64,3696]{1,0:T(8,128)(2,1)S(1)} all-gather(bf16[16,3696]{1,0:T(8,128)(2,1)S(1)} %fusion.15), channel_id=1, replica_groups=mesh['role'=2,'rep'=4,'tp'=4] {'rep'}, dimensions={0}, use_global_device_ids=true | all-gather | bytes 591360 | tf_op jit(solution)/shard_map/all_gather | solution.py:55
  25.2 9.3 %all_gather.11 = bf16[64,2048]{1,0:T(8,128)(2,1)S(1)} all-gather(bf16[16,2048]{1,0:T(8,128)(2,1)} %param.14), channel_id=1, replica_groups=mesh['role'=2,'rep'=4,'tp'=4] {'tp'}, dimensions={0}, use_global_device_ids=true | all-gather | bytes 327680 | tf_op jit(solution)/shard_map/all_gather | solution.py:51
  34.5 12.8 %conditional.1 = (f32[3696,2048]{1,0:T(8,128)}) conditional(s32[]{:T(128)} %convert_element_type.85, () %tuple.14, (bf16[64,3696]{1,0:T(8,128)(2,1)S(1)}, bf16[64,2048]{1,0:T(8,128)(2,1)S(1)}) %tuple.15), branch_computations={%region_1.2_spmd, %region_2.3_spmd} | conditional | flops 968884224 | bytes 31012872 | solution.py:64
  34.5 12.8 %fusion.28 = f32[3696,2048]{1,0:T(8,128)} fusion(bf16[64,3696]{1,0:T(8,128)(2,1)S(1)} %get-tuple-element.4, bf16[64,2048]{1,0:T(8,128)(2,1)S(1)} %get-tuple-element.8), kind=kOutput, calls=%fused_computation.39 | convolution fusion | flops 968884224 | bytes 31012864 | tf_op jit(solution)/shard_map/cond/branch_1_fun/dot_general | solution.py:60
  47.3 54.7 %fusion.24 = (bf16[3696,2048]{1,0:T(8,128)(2,1)}, f32[3696,2048]{1,0:T(8,128)}) fusion(f32[3696,2048]{1,0:T(8,128)} %get-tuple-element.16, f32[3696,2048]{1,0:T(8,128)} %param.17, f32[3696,2048]{1,0:T(8,128)} %param.16, f32[1,3696,2048]{2,1,0:T(8,128)} %param.15), kind=kLoop, calls=%fused_computation.36 | loop fusion | flops 128679936 | bytes 166526976 | tf_op jit(solution)/shard_map/convert_element_type | solution.py:74
  101.9 0.0 copy-start.4
  101.9 0.0 copy-start.1
  101.9 6.8 %collective-permute-start = (bf16[3696,2048]{1,0:T(8,128)(2,1)}, bf16[3696,2048]{1,0:T(8,128)(2,1)}, u32[]{:S(2)}, u32[]{:S(2)}) collective-permute-start(bf16[3696,2048]{1,0:T(8,128)(2,1)} %get-tuple-element.12), channel_id=1, source_target_pairs={{0,16},{1,17},{2,18},{3,19},{4,20},{5,21},{6,22},{7,23},{8,24},{9,... | collective-permute-start | bytes 45416456 | tf_op jit(solution)/shard_map/ppermute | solution.py:19
  108.7 13.1 %fusion.25 = f32[64,2048]{1,0:T(8,128)} fusion(bf16[64,3696]{1,0:T(8,128)(2,1)S(1)} %all_gather.9, f32[1,3696,2048]{2,1,0:T(8,128)} %param.15), kind=kOutput, calls=%fused_computation.37 | convolution fusion | flops 968884224 | bytes 31275008 | tf_op jit(solution)/shard_map/dot_general | solution.py:67
  121.9 0.0 reduce-scatter.3.cloned.1.call-update
  121.9 0.0 reduce-scatter.5.cloned.1.call-start
  121.9 0.0 copy-done.2
  121.9 0.1 fusion.14
  122.0 15.1 %all_gather.10 = bf16[64,3696]{1,0:T(8,128)(2,1)S(1)} all-gather(bf16[16,3696]{1,0:T(8,128)(2,1)S(1)} %fusion.14), channel_id=1, replica_groups=mesh['role'=2,'rep'=4,'tp'=4] {'rep'}, dimensions={0}, use_global_device_ids=true | all-gather | bytes 591360 | tf_op jit(solution)/shard_map/all_gather | solution.py:78
  137.1 0.0 copy-done.3
  137.1 10.8 %reduce-scatter.3.cloned.1.call-done = f32[16,2048]{1,0:T(8,128)} async-done(((f32[64,2048]{1,0:T(8,128)}), f32[16,2048]{1,0:T(8,128)}) %reduce-scatter.3.cloned.1.call-update) | async-done | bytes 131088 | tf_op jit(solution)/shard_map/reduce_scatter | solution.py:66
  147.9 1.1 convolution_multiply_fusion
  149.0 0.0 collective-permute-done
  149.0 8.9 %fusion.3 = f32[64,2048]{1,0:T(8,128)} fusion(bf16[64,3696]{1,0:T(8,128)(2,1)S(1)} %all_gather.10, bf16[3696,2048]{1,0:T(8,128)(2,1)} %get-tuple-element.12, bf16[3696,2048]{1,0:T(8,128)(2,1)} %collective-permute-done, pred[]{:T(512)S(6)} %eq.16), kind=kOutput, calls=%fused_computation.7 | convolution fusion | flops 976453632 | bytes 31275008 | tf_op jit(solution)/shard_map/dot_general | solution.py:80
  157.9 0.0 reduce-scatter.5.cloned.1.call-update
  158.0 27.0 %select_bitcast_fusion = f32[1,3696,2048]{2,1,0:T(8,128)} fusion(f32[3696,2048]{1,0:T(8,128)} %get-tuple-element.13, bf16[3696,2048]{1,0:T(8,128)(2,1)} %collective-permute-done, pred[]{:T(512)S(6)} %eq.16), kind=kLoop, calls=%fused_computation.5 | loop fusion | flops 15138816 | bytes 75694080 | tf_op jit(solution)/shard_map/broadcast_in_dim | solution.py:94
  184.9 1.6 fusion.19
  (9 shorter events, 0.0 us)
Async XLA Ops:
  7.2 140.7 %reduce-scatter.3.cloned.1.call-start = ((), (), s32[]{:S(2)}) async-start(), calls=%async_computation.2 | async-start | bytes 655360 | tf_op jit(solution)/shard_map/reduce_scatter | solution.py:66
  101.9 20.0 %copy-start.2 = (bf16[1,2,16,3696]{3,2,1,0:T(8,128)(2,1)S(1)}, bf16[1,2,16,3696]{3,2,1,0:T(8,128)(2,1)}, u32[]{:S(2)}) copy-start(bf16[1,2,16,3696]{3,2,1,0:T(8,128)(2,1)} %param.12) | copy-start | bytes 709636
  101.9 35.2 %copy-start.3 = (s32[1,16]{1,0:T(1,128)S(1)}, s32[1,16]{1,0:T(1,128)}, u32[]{:S(2)}) copy-start(s32[1,16]{1,0:T(1,128)} %param.19) | copy-start | bytes 196
  101.9 35.2 %copy-start.4 = (s32[1,16]{1,0:T(1,128)S(1)}, s32[1,16]{1,0:T(1,128)}, u32[]{:S(2)}) copy-start(s32[1,16]{1,0:T(1,128)} %param.18) | copy-start | bytes 196
  101.9 46.0 %copy-start.1 = (bf16[1,2,16,2048]{3,2,1,0:T(8,128)(2,1)S(1)}, bf16[1,2,16,2048]{3,2,1,0:T(8,128)(2,1)}, u32[]{:S(2)}) copy-start(bf16[1,2,16,2048]{3,2,1,0:T(8,128)(2,1)} %param.13) | copy-start | bytes 393220
  101.9 47.1 %collective-permute-start = (bf16[3696,2048]{1,0:T(8,128)(2,1)}, bf16[3696,2048]{1,0:T(8,128)(2,1)}, u32[]{:S(2)}, u32[]{:S(2)}) collective-permute-start(bf16[3696,2048]{1,0:T(8,128)(2,1)} %get-tuple-element.12), channel_id=1, source_target_pairs={{0,16},{1,17},{2,18},{3,19},{4,20},{5,21},{6,22},{7,23},{8,24},{9,... | collective-permute-start | bytes 45416456 | tf_op jit(solution)/shard_map/ppermute | solution.py:19
  121.9 63.1 %reduce-scatter.5.cloned.1.call-start = ((), (), s32[]{:S(2)}) async-start(), calls=%async_computation.3 | async-start | bytes 655360 | tf_op jit(solution)/shard_map/reduce_scatter | solution.py:79
  157.9 27.0 %copy-start = (f32[16,2048]{1,0:T(8,128)S(1)}, f32[16,2048]{1,0:T(8,128)}, u32[]{:S(2)}) copy-start(f32[16,2048]{1,0:T(8,128)} %reduce-scatter.3.cloned.1.call-done) | copy-start | bytes 393220
Sparse Core Ops, SparseCore 0:
  122.0 25.8 reduce-scatter.2
  158.1 25.0 reduce-scatter.4
where the time goes:
time: 194 us; the launch traced here: 193 us
  other arithmetic  84.4 us (44%)
  blocking collectives  41.3 us (21%)
  matrix products  35.9 us (19%)
  between operations  14.1 us (7%)
  waiting for transfers between devices  10.8 us (6%)
  starting transfers between devices  6.85 us (4%)
    convert_element_type x1, other arithmetic, local(): fresh = updated.astype(jnp.bfloat16)  54.7 us
    broadcast_in_dim x2, other arithmetic, local(): return (first_out[None], next_out[None], new_weights[None])  28.6 us
    all_gather x1, blocking collectives, local(): segment = lax.all_gather(hidden, 'rep', axis=0, tiled=True)  16.9 us
    all_gather x1, blocking collectives, local(): piece = lax.all_gather(upcoming, 'rep', axis=0, tiled=True)  15.1 us
    dot_general x1, matrix products, local(): jnp.dot(partial_value, older, preferred_element_type=jnp.float32)  13.1 us
    dot_general x1, matrix products, accumulate(): lax.dot_general(segment, cot_rows, (((0,), (0,)), ((), ())), preferred_el...  12.8 us
    reduce_scatter x1, waiting for transfers between devices, local(): lax.psum_scatter(jnp.dot(partial_value, older, preferred_element_type=jnp...  10.8 us
    all_gather x1, blocking collectives, local(): cot_rows = lax.all_gather(cotangent, 'tp', axis=0, tiled=True)  9.28 us
  transfers between devices with their start and end apart: 3, of which 1 were waited for; matrix products, arithmetic and copies ran while one was open for 21% of the time, Pallas kernels for 0%

commit v1 on v0

--- a/solution.py
+++ b/solution.py
@@ -11,6 +11,17 @@
 decay_rate = 0.1
 correct_one = 1.0 - 0.9**60
 correct_two = 1.0 - 0.95**60
+
+
+def gather_by_hops(x, axis, dim):
+    n_dev = lax.axis_size(axis)
+    right = [(i, (i + 1) % n_dev) for i in range(n_dev)]
+    parts = [x]
+    for far in range(1, n_dev):
+        parts = [lax.ppermute(parts[0], axis, right), *parts]
+    whole = jnp.concatenate(parts, axis=dim)
+    offset = (lax.axis_index(axis) + 1) * parts[-1].shape[dim]
+    return jnp.roll(whole, offset, axis=dim)
 
 
 def shifted(value, axis, by):
@@ -75,7 +86,7 @@
     pushed = shifted(fresh, "role", 1)
     current = jnp.where(learner, fresh, pushed)
     new_weights = jnp.where(learner, updated, pushed.astype(jnp.float32))
-    piece = lax.all_gather(upcoming, "rep", axis=0, tiled=True)
+    piece = gather_by_hops(upcoming, "rep", 0)
     next_summed = lax.psum_scatter(
         jnp.dot(piece, current, preferred_element_type=jnp.float32),
         "tp",

time: 194 us -> 195 us (level)
  blocking collectives: 41.3 us -> 26.2 us
  waiting for transfers between devices: 10.8 us -> 24 us
  starting transfers between devices: 6.85 us -> 9.11 us
    all_gather x1 -> x0, blocking collectives: 15.1 us -> none  [local(): piece = lax.all_gather(upcoming, 'rep', axis=0, tiled=True)]
    ppermute x0 -> x3, waiting for transfers between devices: none -> 13.2 us  [gather_by_hops(): parts = [lax.ppermute(parts[0], axis, right), *parts]]
    ppermute x0 -> x3, starting transfers between devices: none -> 2.26 us  [gather_by_hops(): parts = [lax.ppermute(parts[0], axis, right), *parts]]
  transfers between devices with their start and end apart: 3 -> 6, of which waited for: 1 -> 3; matrix products, arithmetic and copies ran while one was open for 21% -> 21% of each run, Pallas kernels for 0% -> 0%
where the time goes in v1:
time: 195 us; the launch traced here: 194 us
  other arithmetic  84.6 us (43%)
  matrix products  36 us (18%)
  blocking collectives  26.2 us (13%)
  waiting for transfers between devices  24 us (12%)
  between operations  14.1 us (7%)
  starting transfers between devices  9.11 us (5%)
    convert_element_type x1, other arithmetic, local(): fresh = updated.astype(jnp.bfloat16)  54.7 us
    broadcast_in_dim x2, other arithmetic, local(): return (first_out[None], next_out[None], new_weights[None])  28.6 us
    all_gather x1, blocking collectives, local(): segment = lax.all_gather(hidden, 'rep', axis=0, tiled=True)  16.9 us
    ppermute x3, waiting for transfers between devices, gather_by_hops(): parts = [lax.ppermute(parts[0], axis, right), *parts]  13.2 us
    dot_general x1, matrix products, local(): jnp.dot(partial_value, older, preferred_element_type=jnp.float32)  13.1 us
    dot_general x1, matrix products, accumulate(): lax.dot_general(segment, cot_rows, (((0,), (0,)), ((), ())), preferred_el...  12.8 us
    reduce_scatter x1, waiting for transfers between devices, local(): lax.psum_scatter(jnp.dot(partial_value, older, preferred_element_type=jnp...  10.7 us
    all_gather x1, blocking collectives, local(): cot_rows = lax.all_gather(cotangent, 'tp', axis=0, tiled=True)  9.28 us
  transfers between devices with their start and end apart: 6, of which 3 were waited for; matrix products, arithmetic and copies ran while one was open for 21% of the time, Pallas kernels for 0%

profile of v1, /device:TPU:0, one launch (start us, length us, event | category | flops | bytes accessed | tf_op | source)
XLA Modules:
  0.0 194.2 jit_solution(6375727286473032811)
XLA Ops:
  7.2 0.0 reduce-scatter.3.cloned.1.call-start
  7.2 1.0 fusion.16
  8.3 16.9 %all_gather.6 = bf16[64,3696]{1,0:T(8,128)(2,1)S(1)} all-gather(bf16[16,3696]{1,0:T(8,128)(2,1)S(1)} %fusion.16), channel_id=1, replica_groups=mesh['role'=2,'rep'=4,'tp'=4] {'rep'}, dimensions={0}, use_global_device_ids=true | all-gather | bytes 591360 | tf_op jit(solution)/shard_map/all_gather | solution.py:66
  25.2 9.3 %all_gather.7 = bf16[64,2048]{1,0:T(8,128)(2,1)S(1)} all-gather(bf16[16,2048]{1,0:T(8,128)(2,1)} %param.14), channel_id=1, replica_groups=mesh['role'=2,'rep'=4,'tp'=4] {'tp'}, dimensions={0}, use_global_device_ids=true | all-gather | bytes 327680 | tf_op jit(solution)/shard_map/all_gather | solution.py:62
  34.5 12.8 %conditional.1 = (f32[3696,2048]{1,0:T(8,128)}) conditional(s32[]{:T(128)} %convert_element_type.85, () %tuple.14, (bf16[64,3696]{1,0:T(8,128)(2,1)S(1)}, bf16[64,2048]{1,0:T(8,128)(2,1)S(1)}) %tuple.15), branch_computations={%region_1.2_spmd, %region_2.3_spmd} | conditional | flops 968884224 | bytes 31012872 | solution.py:75
  34.5 12.8 %fusion.30 = f32[3696,2048]{1,0:T(8,128)} fusion(bf16[64,3696]{1,0:T(8,128)(2,1)S(1)} %get-tuple-element.4, bf16[64,2048]{1,0:T(8,128)(2,1)S(1)} %get-tuple-element.8), kind=kOutput, calls=%fused_computation.49 | convolution fusion | flops 968884224 | bytes 31012864 | tf_op jit(solution)/shard_map/cond/branch_1_fun/dot_general | solution.py:71
  47.3 54.7 %fusion.26 = (bf16[3696,2048]{1,0:T(8,128)(2,1)}, f32[3696,2048]{1,0:T(8,128)}) fusion(f32[3696,2048]{1,0:T(8,128)} %get-tuple-element.16, f32[3696,2048]{1,0:T(8,128)} %param.17, f32[3696,2048]{1,0:T(8,128)} %param.16, f32[1,3696,2048]{2,1,0:T(8,128)} %param.15), kind=kLoop, calls=%fused_computation.46 | loop fusion | flops 128679936 | bytes 166526976 | tf_op jit(solution)/shard_map/convert_element_type | solution.py:85
  102.0 6.8 %collective-permute-start.3 = (bf16[3696,2048]{1,0:T(8,128)(2,1)}, bf16[3696,2048]{1,0:T(8,128)(2,1)}, u32[]{:S(2)}, u32[]{:S(2)}) collective-permute-start(bf16[3696,2048]{1,0:T(8,128)(2,1)} %get-tuple-element.12), channel_id=1, source_target_pairs={{0,16},{1,17},{2,18},{3,19},{4,20},{5,21},{6,22},{7,23},{8,24},{9,... | collective-permute-start | bytes 45416456 | tf_op jit(solution)/shard_map/ppermute | solution.py:30
  108.8 0.1 fusion.15
  108.9 2.2 %collective-permute-start = (bf16[16,3696]{1,0:T(8,128)(2,1)S(1)}, bf16[16,3696]{1,0:T(8,128)(2,1)S(1)}, u32[]{:S(2)}, u32[]{:S(2)}) collective-permute-start(bf16[16,3696]{1,0:T(8,128)(2,1)S(1)} %fusion.15), channel_id=1, source_target_pairs={{0,4},{4,8},{8,12},{12,0},{1,5},{5,9},{9,13},{13,1},{2,6},{6,10},{... | collective-permute-start | bytes 354824 | tf_op jit(solution)/shard_map/ppermute | solution.py:21
  111.0 13.1 %fusion.27 = f32[64,2048]{1,0:T(8,128)} fusion(bf16[64,3696]{1,0:T(8,128)(2,1)S(1)} %all_gather.6, f32[1,3696,2048]{2,1,0:T(8,128)} %param.15), kind=kOutput, calls=%fused_computation.47 | convolution fusion | flops 968884224 | bytes 31275008 | tf_op jit(solution)/shard_map/dot_general | solution.py:78
  124.2 0.0 reduce-scatter.3.cloned.1.call-update
  124.2 0.0 reduce-scatter.5.cloned.1.call-start
  124.3 0.1 collective-permute-start.1
  124.4 6.6 %collective-permute-done.1 = bf16[16,3696]{1,0:T(8,128)(2,1)S(1)} collective-permute-done((bf16[16,3696]{1,0:T(8,128)(2,1)S(1)}, bf16[16,3696]{1,0:T(8,128)(2,1)S(1)}, u32[]{:S(2)}, u32[]{:S(2)}) %collective-permute-start.1) | collective-permute-done | bytes 118304 | tf_op jit(solution)/shard_map/ppermute | solution.py:21
  131.0 6.6 %collective-permute-done.2 = bf16[16,3696]{1,0:T(8,128)(2,1)S(1)} collective-permute-done((bf16[16,3696]{1,0:T(8,128)(2,1)S(1)}, bf16[16,3696]{1,0:T(8,128)(2,1)S(1)}, u32[]{:S(2)}, u32[]{:S(2)}) %collective-permute-start.2) | collective-permute-done | bytes 118304 | tf_op jit(solution)/shard_map/ppermute | solution.py:21
  137.7 0.1 constant_dynamic-update-slice_fusion.4
  137.8 0.1 constant_dynamic-update-slice_fusion
  137.9 10.7 %reduce-scatter.3.cloned.1.call-done = f32[16,2048]{1,0:T(8,128)} async-done(((f32[64,2048]{1,0:T(8,128)}), f32[16,2048]{1,0:T(8,128)}) %reduce-scatter.3.cloned.1.call-update) | async-done | bytes 131088 | tf_op jit(solution)/shard_map/reduce_scatter | solution.py:77
  148.6 1.1 convolution_multiply_fusion
  149.7 9.0 %fusion.3 = f32[64,2048]{1,0:T(8,128)} fusion(bf16[3696,2048]{1,0:T(8,128)(2,1)} %get-tuple-element.12, bf16[3696,2048]{1,0:T(8,128)(2,1)} %collective-permute-done.3, pred[]{:T(512)S(6)} %eq.19, bf16[128,3696]{1,0:T(8,128)(2,1)S(1)} %constant_dynamic-update-slice_fusion, s32[]{:T(128)S(6)} %select_n.28), kind=kOutput, calls=%fused_computation.7 | convolution fusion | flops 976453632 | bytes 31277060 | tf_op jit(solution)/shard_map/dot_general | solution.py:91
  158.7 0.0 reduce-scatter.5.cloned.1.call-update
  158.8 27.0 %select_bitcast_fusion = f32[1,3696,2048]{2,1,0:T(8,128)} fusion(f32[3696,2048]{1,0:T(8,128)} %get-tuple-element.13, bf16[3696,2048]{1,0:T(8,128)(2,1)} %collective-permute-done.3, pred[]{:T(512)S(6)} %eq.19), kind=kLoop, calls=%fused_computation.5 | loop fusion | flops 15138816 | bytes 75694080 | tf_op jit(solution)/shard_map/broadcast_in_dim | solution.py:105
  185.7 1.6 fusion.20
  (22 shorter events, 0.1 us)
Async XLA Ops:
  7.2 141.5 %reduce-scatter.3.cloned.1.call-start = ((), (), s32[]{:S(2)}) async-start(), calls=%async_computation.2 | async-start | bytes 655360 | tf_op jit(solution)/shard_map/reduce_scatter | solution.py:77
  47.2 61.5 %copy-start = (bf16[1,2,16,3696]{3,2,1,0:T(8,128)(2,1)S(1)}, bf16[1,2,16,3696]{3,2,1,0:T(8,128)(2,1)}, u32[]{:S(2)}) copy-start(bf16[1,2,16,3696]{3,2,1,0:T(8,128)(2,1)} %param.12) | copy-start | bytes 709636
  102.0 22.4 %copy-start.3 = (s32[1,16]{1,0:T(1,128)S(1)}, s32[1,16]{1,0:T(1,128)}, u32[]{:S(2)}) copy-start(s32[1,16]{1,0:T(1,128)} %param.19) | copy-start | bytes 196
  102.0 29.0 %copy-start.4 = (s32[1,16]{1,0:T(1,128)S(1)}, s32[1,16]{1,0:T(1,128)}, u32[]{:S(2)}) copy-start(s32[1,16]{1,0:T(1,128)} %param.18) | copy-start | bytes 196
  102.0 46.6 %copy-start.2 = (bf16[1,2,16,2048]{3,2,1,0:T(8,128)(2,1)S(1)}, bf16[1,2,16,2048]{3,2,1,0:T(8,128)(2,1)}, u32[]{:S(2)}) copy-start(bf16[1,2,16,2048]{3,2,1,0:T(8,128)(2,1)} %param.13) | copy-start | bytes 393220
  102.0 47.7 %collective-permute-start.3 = (bf16[3696,2048]{1,0:T(8,128)(2,1)}, bf16[3696,2048]{1,0:T(8,128)(2,1)}, u32[]{:S(2)}, u32[]{:S(2)}) collective-permute-start(bf16[3696,2048]{1,0:T(8,128)(2,1)} %get-tuple-element.12), channel_id=1, source_target_pairs={{0,16},{1,17},{2,18},{3,19},{4,20},{5,21},{6,22},{7,23},{8,24},{9,... | collective-permute-start | bytes 45416456 | tf_op jit(solution)/shard_map/ppermute | solution.py:30
  108.9 15.4 %collective-permute-start = (bf16[16,3696]{1,0:T(8,128)(2,1)S(1)}, bf16[16,3696]{1,0:T(8,128)(2,1)S(1)}, u32[]{:S(2)}, u32[]{:S(2)}) collective-permute-start(bf16[16,3696]{1,0:T(8,128)(2,1)S(1)} %fusion.15), channel_id=1, source_target_pairs={{0,4},{4,8},{8,12},{12,0},{1,5},{5,9},{9,13},{13,1},{2,6},{6,10},{... | collective-permute-start | bytes 354824 | tf_op jit(solution)/shard_map/ppermute | solution.py:21
  124.2 61.5 %reduce-scatter.5.cloned.1.call-start = ((), (), s32[]{:S(2)}) async-start(), calls=%async_computation.3 | async-start | bytes 655360 | tf_op jit(solution)/shard_map/reduce_scatter | solution.py:90
  124.3 6.7 %collective-permute-start.1 = (bf16[16,3696]{1,0:T(8,128)(2,1)S(1)}, bf16[16,3696]{1,0:T(8,128)(2,1)S(1)}, u32[]{:S(2)}, u32[]{:S(2)}) collective-permute-start(bf16[16,3696]{1,0:T(8,128)(2,1)S(1)} %collective-permute-done), channel_id=1, source_target_pairs={{0,4},{4,8},{8,12},{12,0},{1,5},{5,9},{9,13},{13,1},{2,6},{6,10},{... | collective-permute-start | bytes 354824 | tf_op jit(solution)/shard_map/ppermute | solution.py:21
  131.0 6.6 %collective-permute-start.2 = (bf16[16,3696]{1,0:T(8,128)(2,1)S(1)}, bf16[16,3696]{1,0:T(8,128)(2,1)S(1)}, u32[]{:S(2)}, u32[]{:S(2)}) collective-permute-start(bf16[16,3696]{1,0:T(8,128)(2,1)S(1)} %collective-permute-done.1), channel_id=1, source_target_pairs={{0,4},{4,8},{8,12},{12,0},{1,5},{5,9},{9,13},{13,1},{2,6},{6,10},{... | collective-permute-start | bytes 354824 | tf_op jit(solution)/shard_map/ppermute | solution.py:21
  158.7 27.0 %copy-start.1 = (f32[16,2048]{1,0:T(8,128)S(1)}, f32[16,2048]{1,0:T(8,128)}, u32[]{:S(2)}) copy-start(f32[16,2048]{1,0:T(8,128)} %reduce-scatter.3.cloned.1.call-done) | copy-start | bytes 393220
Sparse Core Ops, SparseCore 0:
  124.3 24.2 reduce-scatter.2
  158.9 25.1 reduce-scatter.4
